TPU v7x, 128 devices: a whole 4x4x4 slice. The times are simulated.
128 devices in a mesh: dp: 4 (over z), row: 8 (over x_lo, y), col: 4 (over x_hi, core).
Axes of the slice: x: 4 (x_hi: 2, x_lo: 2; x = x_hi * 2 + x_lo), y: 4, z: 4, core: 2. Of those that a mesh axis runs over, the one named last changes fastest.
Arguments:
- tokens: bfloat16 [32768, 6144], P(('dp', 'row', 'col')), may hold values from -60 to 60
- grads: bfloat16 [32768, 24576], P(('dp', 'row', 'col')), may hold values from -2 to 2
- weight_grad: bfloat16 [6144, 24576], P('row', ('dp', 'col')), may hold values from -0.5 to 0.5
Outputs:
- update: bfloat16 [6144, 24576], P('row', ('dp', 'col'))
All inputs are finite; a program needn't handle non-finite values.
Results may differ from a plain program's by a relative error of at most 0.00065.
The roundings to bfloat16 on the way count: a program that leaves them out, or rounds other values in their place, can miss the bound.
Values may be sent and summed in bfloat16 or wider, within the bound.
No kernel may reach another device: no remote copies, remote signals or barrier semaphores. Data moves between devices by JAX's collectives and lax.ppermute only.
A program may use at most 192 MiB of HBM per device.

v0:
```python
import math
import jax
import jax.numpy as jnp
from jax import lax
from jax.sharding import Mesh
from jax.sharding import PartitionSpec as P

D = 6144
F = 24576
BLOCK = 192
STEPS = 3
ROW = ("row_0", "row_1")
COL = ("col_0", "col_1")
DP_ROW_COL = ("dp", "row_0", "row_1", "col_0", "col_1")
ROW_COL = ("row_0", "row_1", "col_0", "col_1")
DP_COL = ("dp", "col_0", "col_1")
epsilon = 1e-06
damping = 0.01
trust_radius = 0.05


def over_axes(array, axes):
    for axis in axes:
        array = lax.psum(array, axis)
    return array


def newton_inverse(blocks, shift):
    size = blocks.shape[-1]
    identity = jnp.eye(size, dtype=jnp.float32)
    matrix = blocks + shift * identity
    frobenius = jnp.sqrt(jnp.sum(matrix * matrix, axis=(1, 2)))
    iterate = identity[None, :, :] / frobenius[:, None, None]
    for sweep in range(STEPS):
        product = jnp.einsum("nij,njk->nik", matrix, iterate, precision=lax.Precision.HIGHEST)
        iterate = jnp.einsum(
            "nij,njk->nik", iterate, 2.0 * identity - product, precision=lax.Precision.HIGHEST
        )
    return iterate.astype(jnp.bfloat16)


def block_trace(blocks):
    return jnp.sum(jnp.diagonal(blocks, axis1=1, axis2=2))


def on_device(tokens, grads, weight_grad):
    count = tokens.shape[0]
    n_dp = lax.axis_size("dp")
    n_row = lax.axis_size(ROW)
    n_col = lax.axis_size(COL)
    devices_all = n_dp * n_row * n_col
    inverse_count = 1.0 / (count * devices_all)
    blocks_in = D // BLOCK
    blocks_out = F // BLOCK
    per_shard = blocks_out // (n_dp * n_col)
    per_owner = blocks_out // devices_all
    row_blocks = D // n_row // BLOCK
    features = tokens.reshape(count, blocks_in, BLOCK)
    part_in = (
        jnp.einsum("tai,taj->aij", features, features, preferred_element_type=jnp.float32)
        * inverse_count
    )
    received = lax.all_to_all(grads, DP_ROW_COL, split_axis=1, concat_axis=0, tiled=True)
    columns = received.reshape(count * devices_all, per_owner, BLOCK)
    owned_out = (
        jnp.einsum("tai,taj->aij", columns, columns, preferred_element_type=jnp.float32)
        * inverse_count
    )
    summed_in = lax.psum(part_in, DP_ROW_COL)
    owned_in = lax.dynamic_slice_in_dim(summed_in, lax.axis_index(ROW) * row_blocks, row_blocks, 0)
    share_in = block_trace(summed_in) / devices_all
    trace_out, trace_in = (
        over_axes(block_trace(owned_out), DP_ROW_COL),
        over_axes(share_in, DP_ROW_COL),
    )
    ratio = jnp.sqrt((trace_in / D + epsilon) / (trace_out / F + epsilon))
    damp_root = math.sqrt(damping)
    inverse_in = newton_inverse(owned_in, ratio * damp_root)
    inverse_own = newton_inverse(owned_out, damp_root / ratio)
    group_blocks = lax.all_gather(inverse_own, ROW_COL, axis=0, tiled=True)
    inverse_out = lax.dynamic_slice_in_dim(
        group_blocks, lax.axis_index(COL) * per_shard, per_shard, 0
    )
    local_rows, local_cols = weight_grad.shape
    left = jnp.einsum(
        "aij,ajc->aic",
        inverse_in,
        weight_grad.reshape(row_blocks, BLOCK, local_cols),
        preferred_element_type=jnp.float32,
    )
    left = left.reshape(local_rows, local_cols).astype(jnp.bfloat16)
    natural = jnp.einsum(
        "rkj,kji->rki",
        left.reshape(local_rows, per_shard, BLOCK),
        inverse_out,
        preferred_element_type=jnp.float32,
    ).reshape(local_rows, local_cols)
    alignment = over_axes(jnp.sum(natural * weight_grad.astype(jnp.float32)), DP_ROW_COL)
    return (natural * jnp.sqrt(trust_radius * D * F / alignment)).astype(jnp.bfloat16)


def solution(mesh):
    finer = Mesh(
        mesh.devices.reshape(mesh.shape["dp"], 2, 4, 2, 2),
        ("dp", "row_0", "row_1", "col_0", "col_1"),
    )
    placed = (P(DP_ROW_COL, None), P(DP_ROW_COL, None), P(ROW, DP_COL))
    return jax.shard_map(
        on_device, mesh=finer, in_specs=placed, out_specs=P(ROW, DP_COL), check_vma=False
    )
```

profile of v0, /device:TPU:1, one launch (start us, length us, event | category | flops | bytes accessed | tf_op | source)
XLA Modules:
  0.0 519.1 jit_solution(1380360303799974185)
XLA Ops:
  6.5 16.6 %copy.12 = bf16[256,24576]{0,1:T(8,128)(2,1)} copy(bf16[256,24576]{1,0:T(8,128)(2,1)} %param.4) | data formatting | bytes 25165824 | tf_op args[1]
  23.2 11.9 %all-to-all-start = ((bf16[256,128,192]{0,2,1:T(8,128)(2,1)}), bf16[256,128,192]{0,2,1:T(8,128)(2,1)}, u32[]{:S(2)}, u32[]{:S(2)}) async-start(bf16[256,128,192]{0,2,1:T(8,128)(2,1)} %bitcast.37), calls=%async_computation | async-start | bytes 25165824 | tf_op jit(solution)/shard_map/all_to_all | solution.py:63
  35.1 3.2 copy.13
  38.3 3.7 broadcast_multiply_fusion
  42.1 284.1 %all-reduce.7.cloned.1.call-done = f32[32,192,192]{2,1,0:T(8,128)} async-done(((f32[32,192,192]{2,1,0:T(8,128)}), f32[32,192,192]{2,1,0:T(8,128)}) %all-reduce.7.cloned.1.call-update) | async-done | bytes 4718608 | tf_op jit(solution)/shard_map/psum | solution.py:69
  326.2 12.2 %copy.14 = f32[32,192,192]{0,2,1:T(8,128)} copy(f32[32,192,192]{2,1,0:T(8,128)} %all-reduce.7.cloned.1.call-done) | data formatting | bytes 9437184 | tf_op jit(solution)/shard_map/psum | solution.py:69
  338.4 4.6 gather_fusion
  344.3 11.6 %fusion.7 = f32[192,192]{1,0:T(8,128)S(1)} fusion(bf16[256,128,192]{0,2,1:T(8,128)(2,1)} %all-to-all-done), kind=kOutput, calls=%fused_computation.18 | convolution fusion | flops 2415955968 | bytes 12730368 | tf_op jit(solution)/shard_map/tai,taj->aij/dot_general | solution.py:66
  355.9 1.9 gather_fusion.1
  358.4 9.0 %all-reduce.1 = (f32[]{:T(128)}, f32[]{:T(128)}) all-reduce(f32[]{:T(128)S(6)} %div.43, f32[]{:T(128)} %reduce.2), channel_id=1, replica_groups=mesh['dp'=4,'row_0'=2,'row_1'=4,'col_0'=2,'col_1'=2] {'dp'}, use_global_device_ids=true, to_apply=%region_2.3 | all-reduce | flops 2 | bytes 16 | tf_op jit(solution)/shard_map/psum | solution.py:24
  367.4 4.5 all-reduce.4
  371.9 7.8 %all-reduce = (f32[]{:T(128)}, f32[]{:T(128)}) all-reduce(f32[]{:T(128)} %get-tuple-element.13, f32[]{:T(128)} %get-tuple-element.14), channel_id=1, replica_groups=mesh['dp'=4,'row_0'=2,'row_1'=4,'col_0'=2,'col_1'=2] {'row_1'}, use_global_device_ids=true, to_apply=%region_4.5 | all-reduce | flops 2 | bytes 16 | tf_op jit(solution)/shard_map/psum | solution.py:24
  379.7 6.0 %all-reduce.3 = (f32[]{:T(128)}, f32[]{:T(128)}) all-reduce(f32[]{:T(128)} %get-tuple-element.5, f32[]{:T(128)} %get-tuple-element.6), channel_id=1, replica_groups=mesh['dp'=4,'row_0'=2,'row_1'=4,'col_0'=2,'col_1'=2] {'col_0'}, use_global_device_ids=true, to_apply=%region_5.6 | all-reduce | flops 2 | bytes 16 | tf_op jit(solution)/shard_map/psum | solution.py:24
  385.7 10.4 %all-reduce.2 = (f32[]{:T(128)}, f32[]{:T(128)}) all-reduce(f32[]{:T(128)} %get-tuple-element.11, f32[]{:T(128)} %get-tuple-element.12), channel_id=1, replica_groups=mesh['dp'=4,'row_0'=2,'row_1'=4,'col_0'=2,'col_1'=2] {'col_1'}, use_global_device_ids=true, to_apply=%region_6.7 | all-reduce | flops 2 | bytes 16 | tf_op jit(solution)/shard_map/psum | solution.py:24
  400.4 0.9 convolution_convert_fusion.2
  401.5 1.3 multiply_reduce_fusion.1
  402.8 2.1 convolution_subtract_fusion.2
  405.0 0.9 fusion.11
  405.9 2.2 convolution_subtract_fusion.1
  409.1 2.1 convolution_subtract_fusion
  412.0 2.2 convolution_convert_fusion
  414.2 4.7 convert_element_type.38
  419.0 35.9 %all-gather.3.cloned.1.call-done = bf16[6144,192]{1,0:T(8,128)(2,1)} async-done(((bf16[192,192]{1,0:T(8,128)(2,1)}), bf16[6144,192]{1,0:T(8,128)(2,1)}) %all-gather.3.cloned.1.call-update) | async-done | bytes 2359312 | tf_op jit(solution)/shard_map/all_gather | solution.py:80
  454.9 4.8 fusion.2
  459.7 6.3 %copy.18 = f32[768,1536]{1,0:T(8,128)} copy(f32[768,1536]{0,1:T(8,128)} %bitcast.41) | data formatting | bytes 9437184 | tf_op jit(solution)/shard_map/reshape | solution.py:97
  466.0 4.2 multiply_reduce_fusion
  470.1 9.3 %psum.123 = f32[]{:T(128)} all-reduce(f32[]{:T(128)} %multiply_reduce_fusion), channel_id=1, replica_groups=mesh['dp'=4,'row_0'=2,'row_1'=4,'col_0'=2,'col_1'=2] {'dp'}, use_global_device_ids=true, to_apply=%region_16.17 | all-reduce | flops 1 | bytes 8 | tf_op jit(solution)/shard_map/psum | solution.py:24
  479.4 4.4 psum.124
  483.8 8.1 %psum.125 = f32[]{:T(128)} all-reduce(f32[]{:T(128)} %psum.124), channel_id=1, replica_groups=mesh['dp'=4,'row_0'=2,'row_1'=4,'col_0'=2,'col_1'=2] {'row_1'}, use_global_device_ids=true, to_apply=%region_18.19 | all-reduce | flops 1 | bytes 8 | tf_op jit(solution)/shard_map/psum | solution.py:24
  491.9 5.9 %psum.126 = f32[]{:T(128)} all-reduce(f32[]{:T(128)} %psum.125), channel_id=1, replica_groups=mesh['dp'=4,'row_0'=2,'row_1'=4,'col_0'=2,'col_1'=2] {'col_0'}, use_global_device_ids=true, to_apply=%region_19.20 | all-reduce | flops 1 | bytes 8 | tf_op jit(solution)/shard_map/psum | solution.py:24
  497.8 9.4 %psum.127 = f32[]{:T(128)} all-reduce(f32[]{:T(128)} %psum.126), channel_id=1, replica_groups=mesh['dp'=4,'row_0'=2,'row_1'=4,'col_0'=2,'col_1'=2] {'col_1'}, use_global_device_ids=true, to_apply=%region_20.21 | all-reduce | flops 1 | bytes 8 | tf_op jit(solution)/shard_map/psum | solution.py:24
  507.9 4.3 multiply_convert_fusion
  (24 shorter events, 5.5 us)
Async XLA Ops:
  23.2 321.1 %all-to-all-start = ((bf16[256,128,192]{0,2,1:T(8,128)(2,1)}), bf16[256,128,192]{0,2,1:T(8,128)(2,1)}, u32[]{:S(2)}, u32[]{:S(2)}) async-start(bf16[256,128,192]{0,2,1:T(8,128)(2,1)} %bitcast.37), calls=%async_computation | async-start | bytes 25165824 | tf_op jit(solution)/shard_map/all_to_all | solution.py:63
  35.1 291.1 %all-reduce.7.cloned.1.call-start = ((), (), s32[]{:S(2)}) async-start(), calls=%async_computation.1 | async-start | bytes 12582912 | tf_op jit(solution)/shard_map/psum | solution.py:69
  42.0 412.9 %all-gather.3.cloned.1.call-start = ((), (), s32[]{:S(2)}) async-start(), calls=%async_computation.2 | async-start | bytes 3244032 | tf_op jit(solution)/shard_map/all_gather | solution.py:80
  405.9 6.1 %copy-start = (bf16[768,1536]{1,0:T(8,128)(2,1)S(1)}, bf16[768,1536]{1,0:T(8,128)(2,1)}, u32[]{:S(2)}) copy-start(bf16[768,1536]{1,0:T(8,128)(2,1)} %param.5) | copy-start | bytes 7077892
  459.7 6.3 %copy-start.1 = (bf16[768,1536]{1,0:T(8,128)(2,1)S(1)}, bf16[768,1536]{1,0:T(8,128)(2,1)}, u32[]{:S(2)}) copy-start(bf16[768,1536]{1,0:T(8,128)(2,1)} %param.5) | copy-start | bytes 7077892
Sparse Core Ops, SparseCore 0:
  42.1 284.0 all-reduce.6
  401.5 53.3 all-gather.2
where the time goes:
time: 521 us; the launch traced here: 519 us
  waiting for transfers between devices  320 us (61%)
  blocking collectives  74.7 us (14%)
  local copies, waits for them, and re-layouts  49.6 us (10%)
  matrix products  34 us (7%)
  between operations  17 us (3%)
  starting transfers between devices  12 us (2%)
  other arithmetic  11.7 us (2%)
    psum x1, waiting for transfers between devices, on_device(): summed_in = lax.psum(part_in, DP_ROW_COL)  284 us
    psum x10, blocking collectives, over_axes(): array = lax.psum(array, axis)  74.7 us
    all_gather x1, waiting for transfers between devices, on_device(): group_blocks = lax.all_gather(inverse_own, ROW_COL, axis=0, tiled=True)  35.9 us
    unnamed x6, local copies, waits for them, and re-layouts  19.8 us
    psum x1, local copies, waits for them, and re-layouts, on_device(): summed_in = lax.psum(part_in, DP_ROW_COL)  12.2 us
    all_to_all x1, starting transfers between devices, on_device(): lax.all_to_all(grads, DP_ROW_COL, split_axis=1, concat_axis=0, tiled=True)  11.9 us
    dot_general x1, matrix products, on_device(): jnp.einsum('tai,taj->aij', columns, columns, preferred_element_type=jnp.f...  11.6 us
  transfers between devices with their start and end apart: 3, of which 2 were waited for; matrix products, arithmetic and copies ran while one was open for 8% of the time, Pallas kernels for 0%

commit v1 on v0

--- a/solution.py
+++ b/solution.py
@@ -21,7 +21,7 @@
 
 def over_axes(array, axes):
     for axis in axes:
-        array = lax.psum(array, axis)
+        array = jnp.sum(jax.lax.all_gather(array, axis_name=axis), 0)
     return array
 
 

time: 521 us -> 548 us (1.052)
  local copies, waits for them, and re-layouts: 49.6 us -> 73.8 us
  other arithmetic: 11.7 us -> 21.1 us
  blocking collectives: 74.7 us -> 68.1 us
    psum x10 -> x0, blocking collectives: 74.7 us -> none  [over_axes(): array = lax.psum(array, axis)]
    unnamed x0 -> x10, blocking collectives: none -> 68.1 us
    unnamed x6 -> x51, local copies, waits for them, and re-layouts: 19.8 us -> 44.1 us
    reduce_sum x0 -> x15, other arithmetic: none -> 9.35 us  [over_axes(): array = jnp.sum(jax.lax.all_gather(array, axis_name=axis), 0)]
where the time goes in v1:
time: 548 us; the launch traced here: 546 us
  waiting for transfers between devices  320 us (58%)
  local copies, waits for them, and re-layouts  73.8 us (13%)
  blocking collectives  68.1 us (12%)
  matrix products  34.1 us (6%)
  other arithmetic  21.1 us (4%)
  between operations  17.2 us (3%)
  starting transfers between devices  12 us (2%)
    psum x1, waiting for transfers between devices, on_device(): summed_in = lax.psum(part_in, DP_ROW_COL)  284 us
    unnamed x10, blocking collectives  68.1 us
    unnamed x51, local copies, waits for them, and re-layouts  44.1 us
    all_gather x1, waiting for transfers between devices, on_device(): group_blocks = lax.all_gather(inverse_own, ROW_COL, axis=0, tiled=True)  36 us
    psum x1, local copies, waits for them, and re-layouts, on_device(): summed_in = lax.psum(part_in, DP_ROW_COL)  12.2 us
    all_to_all x1, starting transfers between devices, on_device(): lax.all_to_all(grads, DP_ROW_COL, split_axis=1, concat_axis=0, tiled=True)  11.9 us
    dot_general x1, matrix products, on_device(): jnp.einsum('tai,taj->aij', columns, columns, preferred_element_type=jnp.f...  11.6 us
  transfers between devices with their start and end apart: 3, of which 2 were waited for; matrix products, arithmetic and copies ran while one was open for 8% of the time, Pallas kernels for 0%

profile of v1, /device:TPU:1, one launch (start us, length us, event | category | flops | bytes accessed | tf_op | source)
XLA Modules:
  0.0 545.9 jit_solution(639691920309871633)
XLA Ops:
  6.5 16.6 %copy.12 = bf16[256,24576]{0,1:T(8,128)(2,1)} copy(bf16[256,24576]{1,0:T(8,128)(2,1)} %param.4) | data formatting | bytes 25165824 | tf_op args[1]
  23.2 11.9 %all-to-all-start = ((bf16[256,128,192]{0,2,1:T(8,128)(2,1)}), bf16[256,128,192]{0,2,1:T(8,128)(2,1)}, u32[]{:S(2)}, u32[]{:S(2)}) async-start(bf16[256,128,192]{0,2,1:T(8,128)(2,1)} %bitcast.57), calls=%async_computation | async-start | bytes 25165824 | tf_op jit(solution)/shard_map/all_to_all | solution.py:63
  35.1 3.2 copy.13
  38.3 3.7 broadcast_multiply_fusion
  43.2 283.7 %all-reduce.22.cloned.1.call-done = f32[32,192,192]{2,1,0:T(8,128)} async-done(((f32[32,192,192]{2,1,0:T(8,128)}), f32[32,192,192]{2,1,0:T(8,128)}) %all-reduce.22.cloned.1.call-update) | async-done | bytes 4718608 | tf_op jit(solution)/shard_map/psum | solution.py:69
  327.0 12.2 %copy.14 = f32[32,192,192]{0,2,1:T(8,128)} copy(f32[32,192,192]{2,1,0:T(8,128)} %all-reduce.22.cloned.1.call-done) | data formatting | bytes 9437184 | tf_op jit(solution)/shard_map/psum | solution.py:69
  339.2 4.6 gather_fusion
  345.8 11.6 %fusion.7 = f32[192,192]{1,0:T(8,128)S(1)} fusion(bf16[256,128,192]{0,2,1:T(8,128)(2,1)} %all-to-all-done), kind=kOutput, calls=%fused_computation.18 | convolution fusion | flops 2415955968 | bytes 12730368 | tf_op jit(solution)/shard_map/tai,taj->aij/dot_general | solution.py:66
  357.4 1.9 gather_fusion.1
  361.9 8.4 %all-reduce.16 = (f32[4]{0:T(128)S(1)}, f32[4]{0:T(128)S(1)}) all-reduce(f32[4]{0:T(128)S(1)} %dynamic-update-slice, f32[4]{0:T(128)S(1)} %dynamic-update-slice.5), channel_id=1, replica_groups=mesh['dp'=4,'row_0'=2,'row_1'=4,'col_0'=2,'col_1'=2] {'dp'}, use_global_device_ids=true, to_apply=%add | all-reduce | flops 8 | bytes 64
  375.1 3.8 all-reduce.19
  380.1 1.5 dynamic-update-slice.7
  383.7 7.2 %all-reduce.15 = (f32[4]{0:T(128)S(1)}, f32[4]{0:T(128)S(1)}) all-reduce(f32[4]{0:T(128)S(1)} %dynamic-update-slice.2, f32[4]{0:T(128)S(1)} %dynamic-update-slice.7), channel_id=1, replica_groups=mesh['dp'=4,'row_0'=2,'row_1'=4,'col_0'=2,'col_1'=2] {'row_1'}, use_global_device_ids=true, to_apply=%add.2 | all-reduce | flops 8 | bytes 64
  392.1 1.4 dynamic-update-slice.8
  395.6 5.3 all-reduce.18
  402.2 1.5 dynamic-update-slice.9
  405.1 9.7 %all-reduce.17 = (f32[2]{0:T(128)S(1)}, f32[2]{0:T(128)S(1)}) all-reduce(f32[2]{0:T(128)S(1)} %dynamic-update-slice.4, f32[2]{0:T(128)S(1)} %dynamic-update-slice.9), channel_id=1, replica_groups=mesh['dp'=4,'row_0'=2,'row_1'=4,'col_0'=2,'col_1'=2] {'col_1'}, use_global_device_ids=true, to_apply=%add.4 | all-reduce | flops 4 | bytes 32
  422.8 2.1 convolution_subtract_fusion.2
  426.0 2.2 convolution_subtract_fusion.1
  429.1 2.1 convolution_subtract_fusion
  432.1 2.2 convolution_convert_fusion
  434.3 4.7 convert_element_type.38
  439.0 36.0 %all-gather.3.cloned.1.call-done = bf16[6144,192]{1,0:T(8,128)(2,1)} async-done(((bf16[192,192]{1,0:T(8,128)(2,1)}), bf16[6144,192]{1,0:T(8,128)(2,1)}) %all-gather.3.cloned.1.call-update) | async-done | bytes 2359312 | tf_op jit(solution)/shard_map/all_gather | solution.py:80
  475.0 4.9 fusion.2
  479.9 6.2 %copy.18 = f32[768,1536]{1,0:T(8,128)} copy(f32[768,1536]{0,1:T(8,128)} %bitcast.61) | data formatting | bytes 9437184 | tf_op jit(solution)/shard_map/reshape | solution.py:97
  486.0 4.2 multiply_reduce_fusion
  491.6 8.8 %all-reduce.10 = f32[4]{0:T(128)S(1)} all-reduce(f32[4]{0:T(128)S(1)} %dynamic-update-slice.10), channel_id=1, replica_groups=mesh['dp'=4,'row_0'=2,'row_1'=4,'col_0'=2,'col_1'=2] {'dp'}, use_global_device_ids=true, to_apply=%add.10 | all-reduce | flops 4 | bytes 32
  502.3 3.8 all-reduce.11
  508.1 7.3 %all-reduce.12 = f32[4]{0:T(128)S(1)} all-reduce(f32[4]{0:T(128)S(1)} %dynamic-update-slice.12), channel_id=1, replica_groups=mesh['dp'=4,'row_0'=2,'row_1'=4,'col_0'=2,'col_1'=2] {'row_1'}, use_global_device_ids=true, to_apply=%add.12 | all-reduce | flops 4 | bytes 32
  517.4 5.3 all-reduce.13
  524.7 8.7 %all-reduce.14 = f32[2]{0:T(128)S(1)} all-reduce(f32[2]{0:T(128)S(1)} %dynamic-update-slice.14), channel_id=1, replica_groups=mesh['dp'=4,'row_0'=2,'row_1'=4,'col_0'=2,'col_1'=2] {'col_1'}, use_global_device_ids=true, to_apply=%add.14 | all-reduce | flops 2 | bytes 16
  534.8 4.3 multiply_convert_fusion
  (84 shorter events, 38.0 us)
Async XLA Ops:
  23.2 322.6 %all-to-all-start = ((bf16[256,128,192]{0,2,1:T(8,128)(2,1)}), bf16[256,128,192]{0,2,1:T(8,128)(2,1)}, u32[]{:S(2)}, u32[]{:S(2)}) async-start(bf16[256,128,192]{0,2,1:T(8,128)(2,1)} %bitcast.57), calls=%async_computation | async-start | bytes 25165824 | tf_op jit(solution)/shard_map/all_to_all | solution.py:63
  35.1 291.9 %all-reduce.22.cloned.1.call-start = ((), (), s32[]{:S(2)}) async-start(), calls=%async_computation.1 | async-start | bytes 12582912 | tf_op jit(solution)/shard_map/psum | solution.py:69
  42.0 0.7 copy-start.6
  42.0 433.0 %all-gather.3.cloned.1.call-start = ((), (), s32[]{:S(2)}) async-start(), calls=%async_computation.2 | async-start | bytes 3244032 | tf_op jit(solution)/shard_map/all_gather | solution.py:80
  345.8 15.5 %copy-start.5 = (u32[128]{0:T(128)S(1)}, u32[128]{0:T(128)}, u32[]{:S(2)}) copy-start(u32[128]{0:T(128)} %constant.98) | copy-start | bytes 1540
  345.8 28.7 %copy-start.4 = (u32[128]{0:T(128)S(1)}, u32[128]{0:T(128)}, u32[]{:S(2)}) copy-start(u32[128]{0:T(128)} %constant.103) | copy-start | bytes 1540
  345.8 37.3 %copy-start.3 = (u32[128]{0:T(128)S(1)}, u32[128]{0:T(128)}, u32[]{:S(2)}) copy-start(u32[128]{0:T(128)} %constant.108) | copy-start | bytes 1540
  345.8 49.2 %copy-start.2 = (u32[128]{0:T(128)S(1)}, u32[128]{0:T(128)}, u32[]{:S(2)}) copy-start(u32[128]{0:T(128)} %constant.113) | copy-start | bytes 1540
  425.9 6.1 %copy-start = (bf16[768,1536]{1,0:T(8,128)(2,1)S(1)}, bf16[768,1536]{1,0:T(8,128)(2,1)}, u32[]{:S(2)}) copy-start(bf16[768,1536]{1,0:T(8,128)(2,1)} %param.5) | copy-start | bytes 7077892
  479.8 6.2 %copy-start.1 = (bf16[768,1536]{1,0:T(8,128)(2,1)S(1)}, bf16[768,1536]{1,0:T(8,128)(2,1)}, u32[]{:S(2)}) copy-start(bf16[768,1536]{1,0:T(8,128)(2,1)} %param.5) | copy-start | bytes 7077892
Sparse Core Ops, SparseCore 0:
  42.1 284.7 all-reduce.21
  421.5 53.4 all-gather.2
